TPU v7x, 32 devices: a 4x4x1 block of a 4x4x8 slice. The times are simulated.
32 devices in a mesh: data: 1 (over z), dap2: 4 (over y), dap: 8 (over x, core).
Axes of the slice: x: 4, y: 4, z: 1, core: 2. Of those that a mesh axis runs over, the one named last changes fastest.
The devices are a block of a 4x4x8 slice.
Arguments:
- pair_act: float32 [256, 256, 128], P(('data', 'dap'), 'dap2')
- pair_mask: int32 [256, 256], P(('data', 'dap'), 'dap2')
- ln_z: bfloat16 [8, 2, 2, 128], replicated
- w_ab: bfloat16 [8, 2, 128, 512], replicated
- w_g: bfloat16 [8, 2, 128, 128], replicated
- ln_x: bfloat16 [8, 2, 2, 128], replicated
- w_o: bfloat16 [8, 2, 128, 128], replicated
Outputs:
- output: float32 [256, 256, 128], P(('data', 'dap'), 'dap2')
All inputs are finite; a program needn't handle non-finite values.
Results may differ from a plain program's by a relative error of at most 0.00457179.
Values are sent between devices in bfloat16 or wider.
A program may use at most 768 MiB of HBM per device.

v0:
```python
import jax
import jax.numpy as jnp
from jax import lax
from jax.sharding import PartitionSpec as P

LN_EPS = 1e-5


def norm_last(values, params):
    mean = jnp.mean(values, axis=-1, keepdims=True)
    centered = values - mean
    variance = jnp.mean(centered * centered, axis=-1, keepdims=True)
    scaled = centered * lax.rsqrt(variance + LN_EPS)
    return (scaled * params[0].astype(jnp.float32) + params[1].astype(jnp.float32)).astype(jnp.bfloat16)


def norm_chan(values, params):
    mean = jnp.mean(values, axis=-3, keepdims=True)
    centered = values - mean
    variance = jnp.mean(centered * centered, axis=-3, keepdims=True)
    scaled = centered * lax.rsqrt(variance + LN_EPS)
    gain = params[0].astype(jnp.float32)[:, None, None]
    bias = params[1].astype(jnp.float32)[:, None, None]
    return (scaled * gain + bias).astype(jnp.bfloat16)


def project_local(z_norm, keep_mask, w_ab):
    hidden = w_ab.shape[1] // 4
    projected = jnp.einsum("ijd,de->eij", z_norm, w_ab, preferred_element_type=jnp.float32)
    a_proj = (keep_mask * jax.nn.sigmoid(projected[hidden:2 * hidden]) * projected[:hidden]).astype(jnp.bfloat16)
    b_proj = (keep_mask * jax.nn.sigmoid(projected[3 * hidden:]) * projected[2 * hidden:3 * hidden]).astype(jnp.bfloat16)
    return a_proj, b_proj


def finish_local(pair_state, z_norm, x_sum, ln_x, w_g, w_o):
    x_norm = norm_chan(x_sum, ln_x)
    update_val = jnp.einsum("cij,cd->ijd", x_norm, w_o, preferred_element_type=jnp.float32)
    gate_val = jax.nn.sigmoid(jnp.einsum("ijd,de->ije", z_norm, w_g, preferred_element_type=jnp.float32))
    return pair_state + gate_val * update_val


def to_transposed(blocks, row_devs, col_devs):
    hidden, n_rows, n_cols = blocks.shape
    n_full = n_rows * row_devs
    fine_rows = n_full // (row_devs * col_devs)
    stage_one = lax.all_to_all(blocks, "dap2", 1, 2, tiled=True)
    stage_one = stage_one.reshape(hidden, fine_rows, row_devs, col_devs * fine_rows)
    stage_two = lax.all_to_all(stage_one, "dap2", 3, 1, tiled=True)
    stage_three = lax.all_to_all(stage_two, "dap", 2, 1, tiled=True)
    stage_three = stage_three.reshape(hidden, n_full, fine_rows)
    return lax.all_to_all(stage_three, "dap2", 1, 2, tiled=True)


def solution(mesh):
    row_devs = mesh.shape["dap"]
    col_devs = mesh.shape["dap2"]
    pair_spec = P(("data", "dap"), "dap2", None)
    mask_spec = P(("data", "dap"), "dap2")

    def tri_update(pair_state, keep_mask, ln_z, w_ab, w_g, ln_x, w_o, outgoing):
        z_norm = norm_last(pair_state, ln_z)
        a_proj, b_proj = project_local(z_norm, keep_mask, w_ab)
        if outgoing:
            a_rows = lax.all_gather(a_proj, "dap2", axis=2, tiled=True)
            b_rows = lax.all_gather(to_transposed(b_proj, row_devs, col_devs), "dap", axis=2, tiled=True)
            x_sum = jnp.einsum("cik,cjk->cij", a_rows, b_rows, preferred_element_type=jnp.float32)
        else:
            a_cols = lax.all_gather(to_transposed(a_proj, row_devs, col_devs), "dap2", axis=1, tiled=True)
            b_cols = lax.all_gather(b_proj, "dap", axis=1, tiled=True)
            x_sum = jnp.einsum("cki,ckj->cij", a_cols, b_cols, preferred_element_type=jnp.float32)
        return finish_local(pair_state, z_norm, x_sum, ln_x, w_g, w_o)

    def local_stack(pair_act, pair_mask, ln_z, w_ab, w_g, ln_x, w_o):
        keep_mask = pair_mask.astype(jnp.float32)
        pair_state = pair_act
        for layer in range(w_o.shape[0]):
            pair_state = tri_update(pair_state, keep_mask, ln_z[layer, 0], w_ab[layer, 0], w_g[layer, 0], ln_x[layer, 0], w_o[layer, 0], True)
            pair_state = tri_update(pair_state, keep_mask, ln_z[layer, 1], w_ab[layer, 1], w_g[layer, 1], ln_x[layer, 1], w_o[layer, 1], False)
        return pair_state

    return jax.shard_map(local_stack, mesh=mesh, in_specs=(pair_spec, mask_spec, P(), P(), P(), P(), P()), out_specs=pair_spec, check_vma=False)
```

profile of v0, /device:TPU:97, one launch (start us, length us, event | category | flops | bytes accessed | tf_op | source)
XLA Modules:
  0.0 2055.8 jit_solution(1215194582348864530)
XLA Ops:
  29.9 16.5 all_to_all.1057
  47.1 18.6 all_to_all.1058
  85.9 39.8 %all-gather.35.cloned.1.call-done = bf16[128,64,256]{1,2,0:T(8,128)(2,1)} async-done(((bf16[128,64,32]{1,2,0:T(8,128)(2,1)}), bf16[128,64,256]{1,2,0:T(8,128)(2,1)}) %all-gather.35.cloned.1.call-update) | async-done | bytes 4194320 | tf_op jit(solution)/shard_map/all_gather | solution.py:65
  161.5 14.9 all_to_all.1062
  190.5 24.7 %all-gather.37.cloned.1.call-done = bf16[128,256,32]{0,2,1:T(8,128)(2,1)} async-done(((bf16[128,64,32]{0,2,1:T(8,128)(2,1)}), bf16[128,256,32]{0,2,1:T(8,128)(2,1)}) %all-gather.37.cloned.1.call-update) | async-done | bytes 2097168 | tf_op jit(solution)/shard_map/all_gather | solution.py:68
  220.1 26.4 %all-gather.39.cloned.1.call-done = bf16[128,256,64]{0,2,1:T(8,128)(2,1)} async-done(((bf16[128,32,64]{0,2,1:T(8,128)(2,1)}), bf16[128,256,64]{0,2,1:T(8,128)(2,1)}) %all-gather.39.cloned.1.call-update) | async-done | bytes 4194320 | tf_op jit(solution)/shard_map/all_gather | solution.py:69
  285.7 16.5 all_to_all.1065
  302.9 16.4 all_to_all.1066
  339.2 40.4 %all-gather.43.cloned.1.call-done = bf16[128,64,256]{1,2,0:T(8,128)(2,1)} async-done(((bf16[128,64,32]{1,2,0:T(8,128)(2,1)}), bf16[128,64,256]{1,2,0:T(8,128)(2,1)}) %all-gather.43.cloned.1.call-update) | async-done | bytes 4194320 | tf_op jit(solution)/shard_map/all_gather | solution.py:65
  415.4 14.9 all_to_all.1070
  445.7 23.3 %all-gather.45.cloned.1.call-done = bf16[128,256,32]{0,2,1:T(8,128)(2,1)} async-done(((bf16[128,64,32]{0,2,1:T(8,128)(2,1)}), bf16[128,256,32]{0,2,1:T(8,128)(2,1)}) %all-gather.45.cloned.1.call-update) | async-done | bytes 2097168 | tf_op jit(solution)/shard_map/all_gather | solution.py:68
  472.9 27.6 %all-gather.47.cloned.1.call-done = bf16[128,256,64]{0,2,1:T(8,128)(2,1)} async-done(((bf16[128,32,64]{0,2,1:T(8,128)(2,1)}), bf16[128,256,64]{0,2,1:T(8,128)(2,1)}) %all-gather.47.cloned.1.call-update) | async-done | bytes 4194320 | tf_op jit(solution)/shard_map/all_gather | solution.py:69
  539.9 16.5 all_to_all.1073
  557.1 16.4 all_to_all.1074
  594.4 39.0 %all-gather.51.cloned.1.call-done = bf16[128,64,256]{1,2,0:T(8,128)(2,1)} async-done(((bf16[128,64,32]{1,2,0:T(8,128)(2,1)}), bf16[128,64,256]{1,2,0:T(8,128)(2,1)}) %all-gather.51.cloned.1.call-update) | async-done | bytes 4194320 | tf_op jit(solution)/shard_map/all_gather | solution.py:65
  669.9 14.9 all_to_all.1078
  700.9 22.6 %all-gather.53.cloned.1.call-done = bf16[128,256,32]{0,2,1:T(8,128)(2,1)} async-done(((bf16[128,64,32]{0,2,1:T(8,128)(2,1)}), bf16[128,256,32]{0,2,1:T(8,128)(2,1)}) %all-gather.53.cloned.1.call-update) | async-done | bytes 2097168 | tf_op jit(solution)/shard_map/all_gather | solution.py:68
  727.5 27.4 %all-gather.55.cloned.1.call-done = bf16[128,256,64]{0,2,1:T(8,128)(2,1)} async-done(((bf16[128,32,64]{0,2,1:T(8,128)(2,1)}), bf16[128,256,64]{0,2,1:T(8,128)(2,1)}) %all-gather.55.cloned.1.call-update) | async-done | bytes 4194320 | tf_op jit(solution)/shard_map/all_gather | solution.py:69
  794.3 16.5 all_to_all.1081
  811.5 16.4 all_to_all.1082
  849.3 38.5 %all-gather.59.cloned.1.call-done = bf16[128,64,256]{1,2,0:T(8,128)(2,1)} async-done(((bf16[128,64,32]{1,2,0:T(8,128)(2,1)}), bf16[128,64,256]{1,2,0:T(8,128)(2,1)}) %all-gather.59.cloned.1.call-update) | async-done | bytes 4194320 | tf_op jit(solution)/shard_map/all_gather | solution.py:65
  924.3 14.9 all_to_all.1086
  954.5 23.4 %all-gather.61.cloned.1.call-done = bf16[128,256,32]{0,2,1:T(8,128)(2,1)} async-done(((bf16[128,64,32]{0,2,1:T(8,128)(2,1)}), bf16[128,256,32]{0,2,1:T(8,128)(2,1)}) %all-gather.61.cloned.1.call-update) | async-done | bytes 2097168 | tf_op jit(solution)/shard_map/all_gather | solution.py:68
  981.8 27.4 %all-gather.63.cloned.1.call-done = bf16[128,256,64]{0,2,1:T(8,128)(2,1)} async-done(((bf16[128,32,64]{0,2,1:T(8,128)(2,1)}), bf16[128,256,64]{0,2,1:T(8,128)(2,1)}) %all-gather.63.cloned.1.call-update) | async-done | bytes 4194320 | tf_op jit(solution)/shard_map/all_gather | solution.py:69
  1048.7 16.5 all_to_all.1089
  1065.9 16.4 all_to_all.1090
  1103.4 38.8 %all-gather.67.cloned.1.call-done = bf16[128,64,256]{1,2,0:T(8,128)(2,1)} async-done(((bf16[128,64,32]{1,2,0:T(8,128)(2,1)}), bf16[128,64,256]{1,2,0:T(8,128)(2,1)}) %all-gather.67.cloned.1.call-update) | async-done | bytes 4194320 | tf_op jit(solution)/shard_map/all_gather | solution.py:65
  1178.7 14.9 all_to_all.1094
  1208.8 23.4 %all-gather.69.cloned.1.call-done = bf16[128,256,32]{0,2,1:T(8,128)(2,1)} async-done(((bf16[128,64,32]{0,2,1:T(8,128)(2,1)}), bf16[128,256,32]{0,2,1:T(8,128)(2,1)}) %all-gather.69.cloned.1.call-update) | async-done | bytes 2097168 | tf_op jit(solution)/shard_map/all_gather | solution.py:68
  1236.2 27.4 %all-gather.71.cloned.1.call-done = bf16[128,256,64]{0,2,1:T(8,128)(2,1)} async-done(((bf16[128,32,64]{0,2,1:T(8,128)(2,1)}), bf16[128,256,64]{0,2,1:T(8,128)(2,1)}) %all-gather.71.cloned.1.call-update) | async-done | bytes 4194320 | tf_op jit(solution)/shard_map/all_gather | solution.py:69
  1303.1 16.5 all_to_all.1097
  1320.3 16.4 all_to_all.1098
  1357.6 39.0 %all-gather.75.cloned.1.call-done = bf16[128,64,256]{1,2,0:T(8,128)(2,1)} async-done(((bf16[128,64,32]{1,2,0:T(8,128)(2,1)}), bf16[128,64,256]{1,2,0:T(8,128)(2,1)}) %all-gather.75.cloned.1.call-update) | async-done | bytes 4194320 | tf_op jit(solution)/shard_map/all_gather | solution.py:65
  1433.1 14.9 all_to_all.1102
  1463.4 23.2 %all-gather.77.cloned.1.call-done = bf16[128,256,32]{0,2,1:T(8,128)(2,1)} async-done(((bf16[128,64,32]{0,2,1:T(8,128)(2,1)}), bf16[128,256,32]{0,2,1:T(8,128)(2,1)}) %all-gather.77.cloned.1.call-update) | async-done | bytes 2097168 | tf_op jit(solution)/shard_map/all_gather | solution.py:68
  1490.6 27.4 %all-gather.79.cloned.1.call-done = bf16[128,256,64]{0,2,1:T(8,128)(2,1)} async-done(((bf16[128,32,64]{0,2,1:T(8,128)(2,1)}), bf16[128,256,64]{0,2,1:T(8,128)(2,1)}) %all-gather.79.cloned.1.call-update) | async-done | bytes 4194320 | tf_op jit(solution)/shard_map/all_gather | solution.py:69
  1557.4 16.5 all_to_all.1105
  1574.6 16.4 all_to_all.1106
  1611.9 39.0 %all-gather.83.cloned.1.call-done = bf16[128,64,256]{1,2,0:T(8,128)(2,1)} async-done(((bf16[128,64,32]{1,2,0:T(8,128)(2,1)}), bf16[128,64,256]{1,2,0:T(8,128)(2,1)}) %all-gather.83.cloned.1.call-update) | async-done | bytes 4194320 | tf_op jit(solution)/shard_map/all_gather | solution.py:65
  1687.4 14.9 all_to_all.1110
  1717.8 23.2 %all-gather.85.cloned.1.call-done = bf16[128,256,32]{0,2,1:T(8,128)(2,1)} async-done(((bf16[128,64,32]{0,2,1:T(8,128)(2,1)}), bf16[128,256,32]{0,2,1:T(8,128)(2,1)}) %all-gather.85.cloned.1.call-update) | async-done | bytes 2097168 | tf_op jit(solution)/shard_map/all_gather | solution.py:68
  1745.0 27.6 %all-gather.87.cloned.1.call-done = bf16[128,256,64]{0,2,1:T(8,128)(2,1)} async-done(((bf16[128,32,64]{0,2,1:T(8,128)(2,1)}), bf16[128,256,64]{0,2,1:T(8,128)(2,1)}) %all-gather.87.cloned.1.call-update) | async-done | bytes 4194320 | tf_op jit(solution)/shard_map/all_gather | solution.py:69
  1812.0 16.5 all_to_all.1113
  1829.2 16.4 all_to_all.1114
  1866.5 39.0 %all-gather.91.cloned.1.call-done = bf16[128,64,256]{1,2,0:T(8,128)(2,1)} async-done(((bf16[128,64,32]{1,2,0:T(8,128)(2,1)}), bf16[128,64,256]{1,2,0:T(8,128)(2,1)}) %all-gather.91.cloned.1.call-update) | async-done | bytes 4194320 | tf_op jit(solution)/shard_map/all_gather | solution.py:65
  1942.0 14.9 all_to_all.1118
  1972.1 23.5 %all-gather.93.cloned.1.call-done = bf16[128,256,32]{0,2,1:T(8,128)(2,1)} async-done(((bf16[128,64,32]{0,2,1:T(8,128)(2,1)}), bf16[128,256,32]{0,2,1:T(8,128)(2,1)}) %all-gather.93.cloned.1.call-update) | async-done | bytes 2097168 | tf_op jit(solution)/shard_map/all_gather | solution.py:68
  1999.6 27.6 %all-gather.95.cloned.1.call-done = bf16[128,256,64]{0,2,1:T(8,128)(2,1)} async-done(((bf16[128,32,64]{0,2,1:T(8,128)(2,1)}), bf16[128,256,64]{0,2,1:T(8,128)(2,1)}) %all-gather.95.cloned.1.call-update) | async-done | bytes 4194320 | tf_op jit(solution)/shard_map/all_gather | solution.py:69
  (476 shorter events, 935.3 us)
Async XLA Ops:
  6.5 5.0 copy-start
  6.5 5.0 copy-start.18
  6.6 75.9 %all-gather.33.cloned.1.call-start = ((), (), s32[]{:S(2)}) async-start(), calls=%async_computation.64 | async-start | bytes 2621440 | tf_op jit(solution)/shard_map/all_gather | solution.py:64
  14.7 111.0 %all-gather.35.cloned.1.call-start = ((), (), s32[]{:S(2)}) async-start(), calls=%async_computation.65 | async-start | bytes 9437184 | tf_op jit(solution)/shard_map/all_gather | solution.py:65
  65.7 13.6 copy-start.17
  79.3 135.8 %all-gather.37.cloned.1.call-start = ((), (), s32[]{:S(2)}) async-start(), calls=%async_computation.66 | async-start | bytes 2621440 | tf_op jit(solution)/shard_map/all_gather | solution.py:68
  130.8 1.2 copy-start.15
  188.2 58.2 %all-gather.39.cloned.1.call-start = ((), (), s32[]{:S(2)}) async-start(), calls=%async_computation.67 | async-start | bytes 4718592 | tf_op jit(solution)/shard_map/all_gather | solution.py:69
  188.9 146.9 %all-gather.41.cloned.1.call-start = ((), (), s32[]{:S(2)}) async-start(), calls=%async_computation.68 | async-start | bytes 2621440 | tf_op jit(solution)/shard_map/all_gather | solution.py:64
  270.9 108.6 %all-gather.43.cloned.1.call-start = ((), (), s32[]{:S(2)}) async-start(), calls=%async_computation.69 | async-start | bytes 9437184 | tf_op jit(solution)/shard_map/all_gather | solution.py:65
  333.1 135.9 %all-gather.45.cloned.1.call-start = ((), (), s32[]{:S(2)}) async-start(), calls=%async_computation.70 | async-start | bytes 2621440 | tf_op jit(solution)/shard_map/all_gather | solution.py:68
  384.7 1.2 copy-start.8
  442.1 58.4 %all-gather.47.cloned.1.call-start = ((), (), s32[]{:S(2)}) async-start(), calls=%async_computation.71 | async-start | bytes 4718592 | tf_op jit(solution)/shard_map/all_gather | solution.py:69
  442.9 146.9 %all-gather.49.cloned.1.call-start = ((), (), s32[]{:S(2)}) async-start(), calls=%async_computation.72 | async-start | bytes 2621440 | tf_op jit(solution)/shard_map/all_gather | solution.py:64
  518.5 1.2 copy-start.1
  525.1 108.3 %all-gather.51.cloned.1.call-start = ((), (), s32[]{:S(2)}) async-start(), calls=%async_computation.73 | async-start | bytes 9437184 | tf_op jit(solution)/shard_map/all_gather | solution.py:65
  587.0 136.5 %all-gather.53.cloned.1.call-start = ((), (), s32[]{:S(2)}) async-start(), calls=%async_computation.74 | async-start | bytes 2621440 | tf_op jit(solution)/shard_map/all_gather | solution.py:68
  639.2 1.2 copy-start.9
  669.9 27.9 %copy-start.16 = (bf16[8,2,2,128]{3,2,1,0:T(2,128)(2,1)S(1)}, bf16[8,2,2,128]{3,2,1,0:T(2,128)(2,1)}, u32[]{:S(2)}) copy-start(bf16[8,2,2,128]{3,2,1,0:T(2,128)(2,1)} %param.9) | copy-start | bytes 24580
  696.7 58.2 %all-gather.55.cloned.1.call-start = ((), (), s32[]{:S(2)}) async-start(), calls=%async_computation.75 | async-start | bytes 4718592 | tf_op jit(solution)/shard_map/all_gather | solution.py:69
  697.3 147.5 %all-gather.57.cloned.1.call-start = ((), (), s32[]{:S(2)}) async-start(), calls=%async_computation.76 | async-start | bytes 2621440 | tf_op jit(solution)/shard_map/all_gather | solution.py:64
  772.9 1.2 copy-start.2
  779.5 108.3 %all-gather.59.cloned.1.call-start = ((), (), s32[]{:S(2)}) async-start(), calls=%async_computation.77 | async-start | bytes 9437184 | tf_op jit(solution)/shard_map/all_gather | solution.py:65
  841.4 136.5 %all-gather.61.cloned.1.call-start = ((), (), s32[]{:S(2)}) async-start(), calls=%async_computation.78 | async-start | bytes 2621440 | tf_op jit(solution)/shard_map/all_gather | solution.py:68
  893.6 1.2 copy-start.10
  951.0 58.2 %all-gather.63.cloned.1.call-start = ((), (), s32[]{:S(2)}) async-start(), calls=%async_computation.79 | async-start | bytes 4718592 | tf_op jit(solution)/shard_map/all_gather | solution.py:69
  951.7 147.2 %all-gather.65.cloned.1.call-start = ((), (), s32[]{:S(2)}) async-start(), calls=%async_computation.80 | async-start | bytes 2621440 | tf_op jit(solution)/shard_map/all_gather | solution.py:64
  1033.9 108.3 %all-gather.67.cloned.1.call-start = ((), (), s32[]{:S(2)}) async-start(), calls=%async_computation.81 | async-start | bytes 9437184 | tf_op jit(solution)/shard_map/all_gather | solution.py:65
  1095.8 136.5 %all-gather.69.cloned.1.call-start = ((), (), s32[]{:S(2)}) async-start(), calls=%async_computation.82 | async-start | bytes 2621440 | tf_op jit(solution)/shard_map/all_gather | solution.py:68
  1205.4 58.2 %all-gather.71.cloned.1.call-start = ((), (), s32[]{:S(2)}) async-start(), calls=%async_computation.83 | async-start | bytes 4718592 | tf_op jit(solution)/shard_map/all_gather | solution.py:69
  1206.1 146.9 %all-gather.73.cloned.1.call-start = ((), (), s32[]{:S(2)}) async-start(), calls=%async_computation.84 | async-start | bytes 2621440 | tf_op jit(solution)/shard_map/all_gather | solution.py:64
  1288.3 108.3 %all-gather.75.cloned.1.call-start = ((), (), s32[]{:S(2)}) async-start(), calls=%async_computation.85 | async-start | bytes 9437184 | tf_op jit(solution)/shard_map/all_gather | solution.py:65
  1350.2 136.5 %all-gather.77.cloned.1.call-start = ((), (), s32[]{:S(2)}) async-start(), calls=%async_computation.86 | async-start | bytes 2621440 | tf_op jit(solution)/shard_map/all_gather | solution.py:68
  1459.8 58.2 %all-gather.79.cloned.1.call-start = ((), (), s32[]{:S(2)}) async-start(), calls=%async_computation.87 | async-start | bytes 4718592 | tf_op jit(solution)/shard_map/all_gather | solution.py:69
  1460.4 146.9 %all-gather.81.cloned.1.call-start = ((), (), s32[]{:S(2)}) async-start(), calls=%async_computation.88 | async-start | bytes 2621440 | tf_op jit(solution)/shard_map/all_gather | solution.py:64
  1542.7 108.3 %all-gather.83.cloned.1.call-start = ((), (), s32[]{:S(2)}) async-start(), calls=%async_computation.89 | async-start | bytes 9437184 | tf_op jit(solution)/shard_map/all_gather | solution.py:65
  1604.5 136.5 %all-gather.85.cloned.1.call-start = ((), (), s32[]{:S(2)}) async-start(), calls=%async_computation.90 | async-start | bytes 2621440 | tf_op jit(solution)/shard_map/all_gather | solution.py:68
  1657.9 2.2 copy-start.25
  1657.9 2.2 copy-start.26
  1714.2 58.4 %all-gather.87.cloned.1.call-start = ((), (), s32[]{:S(2)}) async-start(), calls=%async_computation.91 | async-start | bytes 4718592 | tf_op jit(solution)/shard_map/all_gather | solution.py:69
  1715.0 147.0 %all-gather.89.cloned.1.call-start = ((), (), s32[]{:S(2)}) async-start(), calls=%async_computation.92 | async-start | bytes 2621440 | tf_op jit(solution)/shard_map/all_gather | solution.py:64
  1791.8 2.2 copy-start.21
  1791.8 2.2 copy-start.22
  1797.2 108.3 %all-gather.91.cloned.1.call-start = ((), (), s32[]{:S(2)}) async-start(), calls=%async_computation.93 | async-start | bytes 9437184 | tf_op jit(solution)/shard_map/all_gather | solution.py:65
  1859.1 136.5 %all-gather.93.cloned.1.call-start = ((), (), s32[]{:S(2)}) async-start(), calls=%async_computation.94 | async-start | bytes 2621440 | tf_op jit(solution)/shard_map/all_gather | solution.py:68
  1912.5 2.2 copy-start.19
  1912.6 2.2 copy-start.29
  1968.8 58.4 %all-gather.95.cloned.1.call-start = ((), (), s32[]{:S(2)}) async-start(), calls=%async_computation.95 | async-start | bytes 4718592 | tf_op jit(solution)/shard_map/all_gather | solution.py:69
  (15 other events, 14.7 us)
Sparse Core Ops, SparseCore 0:
  14.8 38.5 all-gather.32
  79.4 46.2 all-gather.34
  188.4 26.7 all-gather.36
  216.6 29.8 all-gather.38
  271.0 36.0 all-gather.40
  333.3 46.2 all-gather.42
  442.2 26.7 all-gather.44
  470.6 29.8 all-gather.46
  525.3 36.0 all-gather.48
  587.2 46.2 all-gather.50
  696.8 26.7 all-gather.52
  725.0 29.8 all-gather.54
  779.7 36.0 all-gather.56
  841.5 46.2 all-gather.58
  951.1 26.7 all-gather.60
  979.4 29.8 all-gather.62
  1034.0 36.0 all-gather.64
  1095.9 46.2 all-gather.66
  1205.5 26.7 all-gather.68
  1233.8 29.8 all-gather.70
  1288.4 36.0 all-gather.72
  1350.3 46.2 all-gather.74
  1459.9 26.7 all-gather.76
  1488.1 29.8 all-gather.78
  1542.8 36.0 all-gather.80
  1604.7 46.2 all-gather.82
  1714.3 26.7 all-gather.84
  1742.7 29.8 all-gather.86
  1797.4 36.0 all-gather.88
  1859.2 46.2 all-gather.90
  1968.9 26.7 all-gather.92
  1997.3 29.8 all-gather.94
where the time goes:
time: 2070 us; the launch traced here: 2060 us
  blocking collectives  860 us (42%)
  waiting for transfers between devices  726 us (35%)
  local copies, waits for them, and re-layouts  224 us (11%)
  matrix products  173 us (8%)
  other arithmetic  51.3 us (2%)
    all_gather x8, waiting for transfers between devices, tri_update(): lax.all_gather(to_transposed(b_proj, row_devs, col_devs), 'dap', axis=2,...  314 us
    all_to_all x16, blocking collectives, to_transposed(): stage_three = lax.all_to_all(stage_two, 'dap', 2, 1, tiled=True)  253 us
    all_gather x8, waiting for transfers between devices, tri_update(): b_cols = lax.all_gather(b_proj, 'dap', axis=1, tiled=True)  219 us
    all_to_all x16, blocking collectives, to_transposed(): stage_one = lax.all_to_all(blocks, 'dap2', 1, 2, tiled=True)  219 us
    all_to_all x16, blocking collectives, to_transposed(): stage_two = lax.all_to_all(stage_one, 'dap2', 3, 1, tiled=True)  215 us
    all_gather x8, waiting for transfers between devices, tri_update(): lax.all_gather(to_transposed(a_proj, row_devs, col_devs), 'dap2', axis=1,...  187 us
    all_to_all x16, blocking collectives, to_transposed(): return lax.all_to_all(stage_three, 'dap2', 1, 2, tiled=True)  174 us
    all_gather x8, local copies, waits for them, and re-layouts, tri_update(): b_cols = lax.all_gather(b_proj, 'dap', axis=1, tiled=True)  103 us
  transfers between devices with their start and end apart: 32, of which 24 were waited for; matrix products, arithmetic and copies ran while one was open for 7% of the time, Pallas kernels for 0%

commit v1 on v0

v1 whole, which is shorter than its diff:
```python
import functools

import jax
import jax.numpy as jnp
from jax import lax
from jax.experimental import pallas as pl
from jax.experimental.pallas import tpu as pltpu
from jax.sharding import PartitionSpec as P

LN_EPS = 1e-5
MESH = pl.DeviceIdType.MESH
HALVES = 2
LANES = 128
SUB = 8


def sigmoid(v):
    return 1.0 / (1.0 + jnp.exp(-v))


def norm_rows(values, gain, bias):
    mean = jnp.mean(values, axis=0, keepdims=True)
    centered = values - mean
    variance = jnp.mean(centered * centered, axis=0, keepdims=True)
    scaled = centered * lax.rsqrt(variance + LN_EPS)
    return (scaled * gain + bias).astype(jnp.bfloat16)


def kernel(row_devs, col_devs, n_updates, z_in, mask, w_in, w_out, ln, z_out, z_norm, gate, stage, send_ab, recv_ab, a_full, b_full, send_x, recv_x, ab_ssem, ab_rsem, x_ssem, x_rsem, own_sem):
    n_dev = row_devs * col_devs
    chips = row_devs // 2
    per_dev = send_ab.shape[2]
    channels = n_dev * per_dev
    half_lanes = z_in.shape[1] // HALVES
    row = lax.axis_index("dap")
    col = lax.axis_index("dap2")
    me = row * col_devs + col
    chip = row // 2
    core = row % 2

    def peer(step):
        other_core = (core + step % 2) % 2
        other_col = (col + (step // 2) % col_devs) % col_devs
        other_chip = (chip + step // (2 * col_devs)) % chips
        other_row = other_chip * 2 + other_core
        return other_row, other_col

    def greet(step, carry):
        other_row, other_col = peer(step)
        pl.semaphore_signal(pltpu.get_barrier_semaphore(), inc=1, device_id={"dap": other_row, "dap2": other_col}, device_id_type=MESH)
        return carry

    lax.fori_loop(1, n_dev, greet, 0)
    pl.semaphore_wait(pltpu.get_barrier_semaphore(), n_dev - 1)

    def send_all(src, dst, ssem, rsem):
        def one(step, carry):
            other_row, other_col = peer(step)
            pltpu.make_async_remote_copy(
                src_ref=src.at[other_row * col_devs + other_col],
                dst_ref=dst.at[me],
                send_sem=ssem,
                recv_sem=rsem,
                device_id={"dap": other_row, "dap2": other_col},
                device_id_type=MESH,
            ).start()
            return carry

        lax.fori_loop(1, n_dev, one, 0)
        pltpu.make_async_copy(src.at[me], dst.at[me], own_sem).start()
        pltpu.make_async_copy(src.at[me], dst.at[me], own_sem).wait()

    def wait_all(buf, sem):
        part = buf.at[pl.ds(0, n_dev - 1)]
        pltpu.make_async_copy(part, part, sem).wait()

    def project(update, half):
        gain = jnp.broadcast_to(ln[update, 0], (channels, 2 * LANES))
        bias = jnp.broadcast_to(ln[update, 1], (channels, 2 * LANES))
        weights = w_in[update, 0:4 * channels]

        def piece(n, carry):
            lanes = pl.ds(pl.multiple_of(half * half_lanes + n * 2 * LANES, 2 * LANES), 2 * LANES)
            zn = norm_rows(z_out[:, lanes], gain, bias)
            z_norm[:, lanes] = zn
            q = jnp.dot(weights, zn, preferred_element_type=jnp.float32)
            keep = mask[:, lanes]
            a = keep * sigmoid(q[channels:2 * channels]) * q[:channels]
            b = keep * sigmoid(q[3 * channels:]) * q[2 * channels:3 * channels]
            for k in range(2):
                sub = n * 2 + k
                stage[pl.ds(sub, channels, stride=2 * SUB), :] = a[:, k * LANES:(k + 1) * LANES]
                stage[pl.ds(SUB + sub, channels, stride=2 * SUB), :] = b[:, k * LANES:(k + 1) * LANES]
            return carry

        lax.fori_loop(0, half_lanes // (2 * LANES), piece, 0)

        def pack(d, carry):
            rows = per_dev * 2 * SUB
            block = stage[pl.ds(pl.multiple_of(d * rows, rows), rows), :]
            send_ab[half, d] = block.astype(jnp.bfloat16).reshape(per_dev, 2 * SUB, LANES)
            return carry

        lax.fori_loop(0, n_dev, pack, 0)
        send_all(send_ab.at[half], recv_ab.at[half], ab_ssem.at[half], ab_rsem.at[half])

    def make_gate(update):
        weights = w_in[update, 4 * channels:]

        def piece(n, carry):
            lanes = pl.ds(pl.multiple_of(n * 2 * LANES, 2 * LANES), 2 * LANES)
            gate[:, lanes] = sigmoid(jnp.dot(weights, z_norm[:, lanes], preferred_element_type=jnp.float32))
            return carry

        lax.fori_loop(0, z_in.shape[1] // (2 * LANES), piece, 0)

    low = lax.broadcasted_iota(jnp.int32, (SUB, LANES), 1) < LANES // 2

    def swap(v):
        return pltpu.roll(v, LANES // 2, 1)

    def join(first, second):
        return jnp.where(low, first, swap(second)), jnp.where(low, swap(first), second)

    def unpack(half):
        def channel(c, carry):
            for r in range(row_devs):
                for h in range(col_devs // 2):
                    first = recv_ab[half, r * col_devs + 2 * h, c].astype(jnp.float32)
                    second = recv_ab[half, r * col_devs + 2 * h + 1, c].astype(jnp.float32)
                    rows = pl.ds(r * 4 * SUB + half * 2 * SUB, 2 * SUB)
                    cols = pl.ds(h * LANES, LANES)
                    a_full[c, rows, cols] = jnp.concatenate(join(first[:SUB], second[:SUB]), axis=0).astype(jnp.bfloat16)
                    b_full[c, rows, cols] = jnp.concatenate(join(first[SUB:], second[SUB:]), axis=0).astype(jnp.bfloat16)
            return carry

        lax.fori_loop(0, per_dev, channel, 0)

    def contract(outgoing):
        dims = (((1,), (1,)), ((), ())) if outgoing else (((0,), (0,)), ((), ()))

        def channel(c, carry):
            x = lax.dot_general(a_full[c], b_full[c], dims, preferred_element_type=jnp.float32)
            for r in range(row_devs):
                for half in range(HALVES):
                    base = r * 4 * SUB + half * 2 * SUB
                    for h in range(col_devs // 2):
                        cols = slice(h * LANES, (h + 1) * LANES)
                        first, second = join(x[base:base + SUB, cols], x[base + SUB:base + 2 * SUB, cols])
                        send_x[half, r * col_devs + 2 * h, c] = first
                        send_x[half, r * col_devs + 2 * h + 1, c] = second
            return carry

        lax.fori_loop(0, per_dev, channel, 0)
        for half in range(HALVES):
            send_all(send_x.at[half], recv_x.at[half], x_ssem.at[half], x_rsem.at[half])

    def finish(update, half):
        gain = jnp.broadcast_to(ln[update, 2], (channels, LANES))
        bias = jnp.broadcast_to(ln[update, 3], (channels, LANES))
        weights = w_out[update]
        flat = recv_x.at[half].reshape(channels * SUB, LANES)

        def piece(n, carry):
            lanes = pl.ds(pl.multiple_of(half * half_lanes + n * LANES, LANES), LANES)
            x = flat[pl.ds(n, channels, stride=SUB), :]
            y = jnp.dot(weights, norm_rows(x, gain, bias), preferred_element_type=jnp.float32)
            z_out[:, lanes] += gate[:, lanes] * y
            return carry

        lax.fori_loop(0, half_lanes // LANES, piece, 0)

    z_out[...] = z_in[...]
    for half in range(HALVES):
        project(0, half)

    def step(update, outgoing, last):
        make_gate(update)
        for half in range(HALVES):
            wait_all(recv_ab.at[half], ab_rsem.at[half])
            unpack(half)
        contract(outgoing)
        for half in range(HALVES):
            wait_all(recv_x.at[half], x_rsem.at[half])
            finish(update, half)
            wait_all(send_ab.at[half], ab_ssem.at[half])
            if last is None:
                project(update + 1, half)
            else:
                @pl.when(jnp.logical_not(last))
                def _():
                    project(update + 1, half)
        for half in range(HALVES):
            wait_all(send_x.at[half], x_ssem.at[half])

    def layer(i, carry):
        step(2 * i, True, None)
        step(2 * i + 1, False, i == n_updates // 2 - 1)
        return carry

    lax.fori_loop(0, n_updates // 2, layer, 0)


def solution(mesh):
    row_devs = mesh.shape["dap"]
    col_devs = mesh.shape["dap2"]
    n_dev = row_devs * col_devs
    pair_spec = P(("data", "dap"), "dap2", None)
    mask_spec = P(("data", "dap"), "dap2")

    def local_stack(pair_act, pair_mask, ln_z, w_ab, w_g, ln_x, w_o):
        n_rows, n_cols, channels = pair_act.shape
        positions = n_rows * n_cols
        n_updates = w_o.shape[0] * w_o.shape[1]
        per_dev = channels // n_dev
        groups = (HALVES, 2, SUB, n_cols)
        z_t = pair_act.reshape(*groups, channels).transpose(4, 0, 2, 1, 3).reshape(channels, positions)
        mask = pair_mask.astype(jnp.float32).reshape(groups).transpose(0, 2, 1, 3).reshape(1, positions)
        w_in = jnp.concatenate([w_ab, w_g], axis=-1).reshape(n_updates, channels, 5 * channels).swapaxes(1, 2)
        w_out = w_o.reshape(n_updates, channels, channels).swapaxes(1, 2)
        ln = jnp.concatenate([ln_z, ln_x], axis=2).astype(jnp.float32).reshape(n_updates, 4, channels, 1)
        vmem = pl.BlockSpec(memory_space=pltpu.VMEM)
        z_t = pl.pallas_call(
            functools.partial(kernel, row_devs, col_devs, n_updates),
            out_shape=jax.ShapeDtypeStruct((channels, positions), jnp.float32),
            in_specs=[vmem] * 5,
            out_specs=vmem,
            scratch_shapes=[
                pltpu.VMEM((channels, positions), jnp.bfloat16),
                pltpu.VMEM((channels, positions), jnp.float32),
                pltpu.VMEM((channels * 2 * SUB, LANES), jnp.float32),
                pltpu.VMEM((HALVES, n_dev, per_dev, 2 * SUB, LANES), jnp.bfloat16),
                pltpu.VMEM((HALVES, n_dev, per_dev, 2 * SUB, LANES), jnp.bfloat16),
                pltpu.VMEM((per_dev, n_rows * row_devs, n_cols * col_devs), jnp.bfloat16),
                pltpu.VMEM((per_dev, n_rows * row_devs, n_cols * col_devs), jnp.bfloat16),
                pltpu.VMEM((HALVES, n_dev, per_dev, SUB, LANES), jnp.float32),
                pltpu.VMEM((HALVES, n_dev, per_dev, SUB, LANES), jnp.float32),
                pltpu.SemaphoreType.DMA((HALVES,)),
                pltpu.SemaphoreType.DMA((HALVES,)),
                pltpu.SemaphoreType.DMA((HALVES,)),
                pltpu.SemaphoreType.DMA((HALVES,)),
                pltpu.SemaphoreType.DMA,
            ],
            compiler_params=pltpu.CompilerParams(collective_id=0, has_side_effects=True, vmem_limit_bytes=40 * 2**20),
        )(z_t, mask, w_in, w_out, ln)
        z = z_t.reshape(channels, HALVES, SUB, 2, n_cols).transpose(1, 3, 2, 4, 0)
        return z.reshape(n_rows, n_cols, channels)

    return jax.shard_map(local_stack, mesh=mesh, in_specs=(pair_spec, mask_spec, P(), P(), P(), P(), P()), out_specs=pair_spec, check_vma=False)
```

time: 2070 us -> 557 us (0.27)
  blocking collectives: 860 us -> 0 us
  waiting for transfers between devices: 726 us -> 0 us
  Pallas kernels: 0 us -> 533 us
  local copies, waits for them, and re-layouts: 224 us -> 18.9 us
  matrix products: 173 us -> 0 us
  other arithmetic: 51.3 us -> 4.3 us
    all_to_all x64 -> x0, blocking collectives: 860 us -> none  [the longest x16 253 us: to_transposed(): stage_three = lax.all_to_all(stage_two, 'dap', 2, 1, tiled=True)]
    all_gather x32 -> x0, waiting for transfers between devices: 720 us -> none  [the longest x8 314 us: tri_update(): lax.all_gather(to_transposed(b_proj, row_devs, col_devs), 'dap', axis=2,...]
    pallas_call x0 -> x1, Pallas kernels: none -> 533 us  [local_stack(): pl.pallas_call(functools.partial(kernel, row_devs, col_devs, n_updates),...]
    dot_general x64 -> x0, matrix products: 173 us -> none  [the longest x8 42.2 us: tri_update(): jnp.einsum('cik,cjk->cij', a_rows, b_rows, preferred_element_type=jnp.flo...]
    all_gather x24 -> x0, local copies, waits for them, and re-layouts: 169 us -> none  [the longest x8 103 us: tri_update(): b_cols = lax.all_gather(b_proj, 'dap', axis=1, tiled=True)]
    all_to_all x64 -> x0, local copies, waits for them, and re-layouts: 39.6 us -> none  [the longest x16 27.7 us: to_transposed(): return lax.all_to_all(stage_three, 'dap2', 1, 2, tiled=True)]
    convert_element_type x37 -> x2, other arithmetic: 32.5 us -> 2.48 us  [the longest x1 2.48 us: local_stack(): jnp.concatenate([ln_z, ln_x], axis=2).astype(jnp.float32)]
  transfers between devices with their start and end apart: 32 -> 0, of which waited for: 24 -> 0; matrix products, arithmetic and copies ran while one was open for 7% -> 0% of each run, Pallas kernels for 0% -> 0%
where the time goes in v1:
time: 557 us; the launch traced here: 556 us
  Pallas kernels  533 us (96%)
  local copies, waits for them, and re-layouts  18.9 us (3%)
    pallas_call x1, Pallas kernels, local_stack(): pl.pallas_call(functools.partial(kernel, row_devs, col_devs, n_updates),...  533 us

profile of v1, /device:TPU:97, one launch (start us, length us, event | category | flops | bytes accessed | tf_op | source)
XLA Modules:
  0.0 556.2 jit_solution(7071937139934952924)
XLA Ops:
  0.0 1.2 copy.51
  1.2 1.2 copy.52
  2.4 0.0 copy-start.3
  2.4 0.0 copy-start.4
  2.4 2.5 maximum_convert_fusion.ln
  4.9 0.0 copy-done.3
  4.9 0.0 copy-done.4
  4.9 1.8 pad_maximum_fusion
  6.7 3.2 copy.47
  10.0 0.0 copy-start.5
  10.0 2.3 copy.45
  12.3 2.5 copy.53.z_in
  14.8 1.3 copy.48
  16.2 0.0 copy-done.5
  16.2 0.1 reshape.57.mask
  16.3 0.0 copy-start
  16.3 2.2 copy-done
  18.5 0.0 copy-start.1
  18.5 1.2 copy-done.1
  19.7 532.9 %shard_map.73 = f32[128,2048]{1,0:T(8,128)S(1)} custom-call(f32[128,2048]{1,0:T(8,128)S(1)} %copy-done.1, f32[1,2048]{1,0:T(1,128)S(1)} %reshape.57.mask, bf16[16,640,128]{2,1,0:T(8,128)(2,1)S(1)} %bitcast.20, bf16[16,128,128]{2,1,0:T(8,128)(2,1)S(1)} %bitcast.21, f32[16,4,128,1]{3,2,1,0:T(8,128)S(1)} %copy-done), custom_call_target="tpu_custom_call" | custom-call | tf_op jit(solution)/shard_map/pallas_call | solution.py:223
  552.6 0.0 copy-start.2
  552.6 1.0 copy-done.2
  553.6 1.6 copy.54
  555.1 1.1 copy.55
  (2 shorter events, 0.0 us)
Async XLA Ops:
  2.4 2.5 copy-start.3
  2.4 2.5 copy-start.4
  10.0 6.2 %copy-start.5 = (s32[32,64]{1,0:T(8,128)S(1)}, s32[32,64]{1,0:T(8,128)}, u32[]{:S(2)}) copy-start(s32[32,64]{1,0:T(8,128)} %param.8) | copy-start | bytes 24580
  16.3 2.2 copy-start
  18.5 1.2 copy-start.1
  552.6 1.0 copy-start.2

commit v2 on v1

v2 whole, which is shorter than its diff:
```python
import functools

import jax
import jax.numpy as jnp
from jax import lax
from jax.experimental import pallas as pl
from jax.experimental.pallas import tpu as pltpu
from jax.sharding import PartitionSpec as P

LN_EPS = 1e-5
MESH = pl.DeviceIdType.MESH
HALVES = 2
LANES = 128
SUB = 8


def norm_rows(values, gain, bias):
    mean = jnp.mean(values, axis=0, keepdims=True)
    centered = values - mean
    variance = jnp.mean(centered * centered, axis=0, keepdims=True)
    scaled = centered * lax.rsqrt(variance + LN_EPS)
    return (scaled * gain + bias).astype(jnp.bfloat16)


def peer_offsets(chips, cols):
    offsets = [(x, y, c) for x in range(chips) for y in range(cols) for c in range(2)][1:]
    return sorted(offsets, key=lambda o: (-min(o[0], chips - o[0]) - min(o[1], cols - o[1]), o[2]))


def kernel(row_devs, col_devs, n_updates, z_in, mask, w_in, w_out, ln, z_out, z_norm, gate, stage, send_ab, recv_ab, a_full, b_full, send_x, recv_x, ab_ssem, ab_rsem, x_ssem, x_rsem):
    n_dev = row_devs * col_devs
    chips = row_devs // 2
    per_dev = send_ab.shape[2]
    channels = n_dev * per_dev
    half_lanes = z_in.shape[1] // HALVES
    wide = 2 * LANES
    part = per_dev // 2
    ab_groups = ((0, 0, per_dev), (1, 0, part), (1, part, part))
    x_groups = ((0, 0, part), (0, part, part), (1, 0, per_dev))
    row = lax.axis_index("dap")
    col = lax.axis_index("dap2")
    me = row * col_devs + col
    chip = row // 2
    core = row % 2
    peers = []
    for x, y, c in peer_offsets(chips, col_devs):
        other_row = (chip + x) % chips * 2 + (core + c) % 2
        peers.append((other_row, (col + y) % col_devs))

    for other_row, other_col in peers:
        pl.semaphore_signal(pltpu.get_barrier_semaphore(), inc=1, device_id={"dap": other_row, "dap2": other_col}, device_id_type=MESH)
    pl.semaphore_wait(pltpu.get_barrier_semaphore(), n_dev - 1)

    def send_group(src, dst, ssem, rsem, groups, g):
        half, first, count = groups[g]
        part_of = pl.ds(first, count)
        for other_row, other_col in peers:
            pltpu.make_async_remote_copy(
                src_ref=src.at[half, other_row * col_devs + other_col, part_of],
                dst_ref=dst.at[half, me, part_of],
                send_sem=ssem.at[g],
                recv_sem=rsem.at[g],
                device_id={"dap": other_row, "dap2": other_col},
                device_id_type=MESH,
            ).start()
        pltpu.make_async_copy(src.at[half, me, part_of], dst.at[half, me, part_of], rsem.at[g]).start()

    def wait_group(buf, sem, groups, g, blocks):
        half, first, count = groups[g]
        whole = buf.at[half, pl.ds(0, blocks), pl.ds(first, count)]
        pltpu.make_async_copy(whole, whole, sem.at[g]).wait()

    def project(update, half):
        gain = jnp.broadcast_to(ln[update, 0], (channels, wide))
        bias = jnp.broadcast_to(ln[update, 1], (channels, wide))
        weights = w_in[update, 0:4 * channels]
        for n in range(half_lanes // wide):
            lanes = pl.ds(half * half_lanes + n * wide, wide)
            zn = norm_rows(z_out[:, lanes], gain, bias)
            z_norm[:, lanes] = zn
            q = jnp.dot(weights, zn, preferred_element_type=jnp.float32)
            keep = 0.5 * mask[:, lanes]
            a = (jnp.tanh(0.5 * q[channels:2 * channels]) + 1.0) * (keep * q[:channels])
            b = (jnp.tanh(0.5 * q[3 * channels:]) + 1.0) * (keep * q[2 * channels:3 * channels])
            for k in range(2):
                sub = n * 2 + k
                stage[pl.ds(sub, channels, stride=2 * SUB), :] = a[:, k * LANES:(k + 1) * LANES]
                stage[pl.ds(SUB + sub, channels, stride=2 * SUB), :] = b[:, k * LANES:(k + 1) * LANES]

        rows = per_dev * 2 * SUB
        for d in range(n_dev):
            send_ab[half, d] = stage[d * rows:(d + 1) * rows, :].astype(jnp.bfloat16).reshape(per_dev, 2 * SUB, LANES)

    def make_gate(update):
        weights = w_in[update, 4 * channels:]

        def piece(n, carry):
            lanes = pl.ds(pl.multiple_of(n * wide, wide), wide)
            v = jnp.dot(weights, z_norm[:, lanes], preferred_element_type=jnp.float32)
            gate[:, lanes] = 0.5 * jnp.tanh(0.5 * v) + 0.5
            return carry

        lax.fori_loop(0, z_in.shape[1] // wide, piece, 0, unroll=4)

    low = lax.broadcasted_iota(jnp.int32, (SUB, LANES), 1) < LANES // 2

    def swap(v):
        return pltpu.roll(v, LANES // 2, 1)

    def join(first, second):
        return jnp.where(low, first, swap(second)), jnp.where(low, swap(first), second)

    def unpack(g):
        half, start, count = ab_groups[g]

        def channel(c, carry):
            for r in range(row_devs):
                for h in range(col_devs // 2):
                    first = recv_ab[half, r * col_devs + 2 * h, c].astype(jnp.float32)
                    second = recv_ab[half, r * col_devs + 2 * h + 1, c].astype(jnp.float32)
                    rows = pl.ds(r * 4 * SUB + half * 2 * SUB, 2 * SUB)
                    cols = pl.ds(h * LANES, LANES)
                    a_full[c, rows, cols] = jnp.concatenate(join(first[:SUB], second[:SUB]), axis=0).astype(jnp.bfloat16)
                    b_full[c, rows, cols] = jnp.concatenate(join(first[SUB:], second[SUB:]), axis=0).astype(jnp.bfloat16)
            return carry

        lax.fori_loop(start, start + count, channel, 0)

    def contract(outgoing, start, count):
        dims = (((1,), (1,)), ((), ())) if outgoing else (((0,), (0,)), ((), ()))
        for c in range(start, start + count):
            x = lax.dot_general(a_full[c], b_full[c], dims, preferred_element_type=jnp.float32)
            for r in range(row_devs):
                for half in range(HALVES):
                    base = r * 4 * SUB + half * 2 * SUB
                    for h in range(col_devs // 2):
                        cols = slice(h * LANES, (h + 1) * LANES)
                        first, second = join(x[base:base + SUB, cols], x[base + SUB:base + 2 * SUB, cols])
                        send_x[half, r * col_devs + 2 * h, c] = first
                        send_x[half, r * col_devs + 2 * h + 1, c] = second

    def finish(update, half):
        gain = jnp.broadcast_to(ln[update, 2], (channels, wide))
        bias = jnp.broadcast_to(ln[update, 3], (channels, wide))
        weights = w_out[update]
        flat = recv_x.at[half].reshape(channels * SUB, LANES)
        for n in range(half_lanes // wide):
            lanes = pl.ds(half * half_lanes + n * wide, wide)
            x = jnp.concatenate([flat[pl.ds(2 * n + k, channels, stride=SUB), :] for k in range(2)], axis=1)
            y = jnp.dot(weights, norm_rows(x, gain, bias), preferred_element_type=jnp.float32)
            z_out[:, lanes] += gate[:, lanes] * y

    z_out[...] = z_in[...]

    def turn(update):
        make_gate(update)
        wait_group(recv_ab, ab_rsem, ab_groups, 0, n_dev)
        unpack(0)
        for g in range(2):
            wait_group(recv_ab, ab_rsem, ab_groups, 1 + g, n_dev)
            unpack(1 + g)
            @pl.when(update % 2 == 0)
            def _():
                contract(True, g * part, part)

            @pl.when(update % 2 == 1)
            def _():
                contract(False, g * part, part)

            send_group(send_x, recv_x, x_ssem, x_rsem, x_groups, g)
        send_group(send_x, recv_x, x_ssem, x_rsem, x_groups, 2)

    def step(i, carry):
        pl.when(i > 0)(lambda: turn(i - 1))
        for half in range(HALVES):
            @pl.when(i > 0)
            def _():
                for g in range(3):
                    if x_groups[g][0] == half:
                        wait_group(recv_x, x_rsem, x_groups, g, n_dev)
                finish(i - 1, half)
                for g in range(3):
                    if ab_groups[g][0] == half:
                        wait_group(send_ab, ab_ssem, ab_groups, g, n_dev - 1)

            @pl.when(i < n_updates)
            def _():
                project(i, half)
                for g in range(3):
                    if ab_groups[g][0] == half:
                        send_group(send_ab, recv_ab, ab_ssem, ab_rsem, ab_groups, g)

        @pl.when(i > 0)
        def _():
            for g in range(3):
                wait_group(send_x, x_ssem, x_groups, g, n_dev - 1)

        return carry

    lax.fori_loop(0, n_updates + 1, step, 0)


def solution(mesh):
    row_devs = mesh.shape["dap"]
    col_devs = mesh.shape["dap2"]
    n_dev = row_devs * col_devs
    pair_spec = P(("data", "dap"), "dap2", None)
    mask_spec = P(("data", "dap"), "dap2")

    def local_stack(pair_act, pair_mask, ln_z, w_ab, w_g, ln_x, w_o):
        n_rows, n_cols, channels = pair_act.shape
        positions = n_rows * n_cols
        n_updates = w_o.shape[0] * w_o.shape[1]
        per_dev = channels // n_dev
        groups = (HALVES, 2, SUB, n_cols)
        z_t = pair_act.reshape(*groups, channels).transpose(4, 0, 2, 1, 3).reshape(channels, positions)
        mask = pair_mask.astype(jnp.float32).reshape(groups).transpose(0, 2, 1, 3).reshape(1, positions)
        w_in = jnp.concatenate([w_ab, w_g], axis=-1).reshape(n_updates, channels, 5 * channels).swapaxes(1, 2)
        w_out = w_o.reshape(n_updates, channels, channels).swapaxes(1, 2)
        ln = jnp.concatenate([ln_z, ln_x], axis=2).astype(jnp.float32).reshape(n_updates, 4, channels, 1)
        vmem = pl.BlockSpec(memory_space=pltpu.VMEM)
        z_t = pl.pallas_call(
            functools.partial(kernel, row_devs, col_devs, n_updates),
            out_shape=jax.ShapeDtypeStruct((channels, positions), jnp.float32),
            in_specs=[vmem] * 5,
            out_specs=vmem,
            scratch_shapes=[
                pltpu.VMEM((channels, positions), jnp.bfloat16),
                pltpu.VMEM((channels, positions), jnp.float32),
                pltpu.VMEM((channels * 2 * SUB, LANES), jnp.float32),
                pltpu.VMEM((HALVES, n_dev, per_dev, 2 * SUB, LANES), jnp.bfloat16),
                pltpu.VMEM((HALVES, n_dev, per_dev, 2 * SUB, LANES), jnp.bfloat16),
                pltpu.VMEM((per_dev, n_rows * row_devs, n_cols * col_devs), jnp.bfloat16),
                pltpu.VMEM((per_dev, n_rows * row_devs, n_cols * col_devs), jnp.bfloat16),
                pltpu.VMEM((HALVES, n_dev, per_dev, SUB, LANES), jnp.float32),
                pltpu.VMEM((HALVES, n_dev, per_dev, SUB, LANES), jnp.float32),
                pltpu.SemaphoreType.DMA((3,)),
                pltpu.SemaphoreType.DMA((3,)),
                pltpu.SemaphoreType.DMA((3,)),
                pltpu.SemaphoreType.DMA((3,)),
            ],
            compiler_params=pltpu.CompilerParams(collective_id=0, has_side_effects=True, vmem_limit_bytes=40 * 2**20),
        )(z_t, mask, w_in, w_out, ln)
        z = z_t.reshape(channels, HALVES, SUB, 2, n_cols).transpose(1, 3, 2, 4, 0)
        return z.reshape(n_rows, n_cols, channels)

    return jax.shard_map(local_stack, mesh=mesh, in_specs=(pair_spec, mask_spec, P(), P(), P(), P(), P()), out_specs=pair_spec, check_vma=False)
```

time: 557 us -> 458 us (0.82)
  Pallas kernels: 533 us -> 435 us
    pallas_call x1, Pallas kernels: 533 us -> 435 us  [local_stack(): pl.pallas_call(functools.partial(kernel, row_devs, col_devs, n_updates),...]
where the time goes in v2:
time: 458 us
  Pallas kernels  435 us (95%)
  local copies, waits for them, and re-layouts  18.9 us (4%)
    pallas_call x1, Pallas kernels, local_stack(): pl.pallas_call(functools.partial(kernel, row_devs, col_devs, n_updates),...  435 us

profile of v2, /device:TPU:97, one launch (start us, length us, event | category | flops | bytes accessed | tf_op | source)
XLA Modules:
  0.0 458.1 jit_solution(13646868849229008038)
XLA Ops:
  0.0 1.2 copy.51
  1.2 1.2 copy.52
  2.4 0.0 copy-start.3
  2.4 0.0 copy-start.4
  2.4 2.5 maximum_convert_fusion.ln
  4.9 0.0 copy-done.3
  4.9 0.0 copy-done.4
  4.9 1.8 pad_maximum_fusion
  6.7 3.2 copy.47
  10.0 0.0 copy-start.5
  10.0 2.3 copy.45
  12.3 2.5 copy.53.z_in
  14.8 1.3 copy.48
  16.2 0.0 copy-done.5
  16.2 0.1 reshape.57.mask
  16.3 0.0 copy-start
  16.3 2.2 copy-done
  18.5 0.0 copy-start.1
  18.5 1.2 copy-done.1
  19.7 434.7 %shard_map.73 = f32[128,2048]{1,0:T(8,128)S(1)} custom-call(f32[128,2048]{1,0:T(8,128)S(1)} %copy-done.1, f32[1,2048]{1,0:T(1,128)S(1)} %reshape.57.mask, bf16[16,640,128]{2,1,0:T(8,128)(2,1)S(1)} %bitcast.20, bf16[16,128,128]{2,1,0:T(8,128)(2,1)S(1)} %bitcast.21, f32[16,4,128,1]{3,2,1,0:T(8,128)S(1)} %copy-done), custom_call_target="tpu_custom_call" | custom-call | tf_op jit(solution)/shard_map/pallas_call | solution.py:222
  454.4 0.0 copy-start.2
  454.5 1.0 copy-done.2
  455.4 1.6 copy.54
  457.0 1.1 copy.55
  (2 shorter events, 0.0 us)
Async XLA Ops:
  2.4 2.5 copy-start.3
  2.4 2.5 copy-start.4
  10.0 6.2 %copy-start.5 = (s32[32,64]{1,0:T(8,128)S(1)}, s32[32,64]{1,0:T(8,128)}, u32[]{:S(2)}) copy-start(s32[32,64]{1,0:T(8,128)} %param.8) | copy-start | bytes 24580
  16.3 2.2 copy-start
  18.5 1.2 copy-start.1
  454.4 1.0 copy-start.2

commit v3 on v2

--- a/solution.py
+++ b/solution.py
@@ -24,15 +24,19 @@
 
 def peer_offsets(chips, cols):
     offsets = [(x, y, c) for x in range(chips) for y in range(cols) for c in range(2)][1:]
-    return sorted(offsets, key=lambda o: (-min(o[0], chips - o[0]) - min(o[1], cols - o[1]), o[2]))
-
-
-def kernel(row_devs, col_devs, n_updates, z_in, mask, w_in, w_out, ln, z_out, z_norm, gate, stage, send_ab, recv_ab, a_full, b_full, send_x, recv_x, ab_ssem, ab_rsem, x_ssem, x_rsem):
+    hx=lambda o: min(o[0], chips - o[0])
+    hy=lambda o: min(o[1], cols - o[1])
+    return sorted(offsets, key=lambda o: (-o[2], -hy(o), -hx(o)))
+
+
+def kernel(row_devs, col_devs, n_updates, z_hbm, mask_in, ln_z, w_ab_hbm, w_g_hbm, ln_x, w_o_hbm, out_hbm, z_raw, w_ab, w_g, w_o, w_in, w_out, ln, mask, z_out, z_norm, gate, stage, send_ab, recv_ab, a_full, b_full, send_x, recv_x, ab_ssem, ab_rsem, x_ssem, x_rsem, z_sem, w_sem):
     n_dev = row_devs * col_devs
     chips = row_devs // 2
     per_dev = send_ab.shape[2]
     channels = n_dev * per_dev
-    half_lanes = z_in.shape[1] // HALVES
+    half_lanes = z_out.shape[1] // HALVES
+    half_rows = z_raw.shape[0] // HALVES
+    n_cols = z_raw.shape[1]
     wide = 2 * LANES
     part = per_dev // 2
     ab_groups = ((0, 0, per_dev), (1, 0, part), (1, part, part))
@@ -49,7 +53,11 @@
 
     for other_row, other_col in peers:
         pl.semaphore_signal(pltpu.get_barrier_semaphore(), inc=1, device_id={"dap": other_row, "dap2": other_col}, device_id_type=MESH)
-    pl.semaphore_wait(pltpu.get_barrier_semaphore(), n_dev - 1)
+
+    z_copies = [pltpu.make_async_copy(z_hbm.at[pl.ds(h * half_rows, half_rows)], z_raw.at[pl.ds(h * half_rows, half_rows)], z_sem.at[h]) for h in range(HALVES)]
+    w_copies = [pltpu.make_async_copy(src, dst, w_sem.at[k]) for k, (src, dst) in enumerate(((w_ab_hbm, w_ab), (w_g_hbm, w_g), (w_o_hbm, w_o)))]
+    for copy in z_copies + w_copies:
+        copy.start()
 
     def send_group(src, dst, ssem, rsem, groups, g):
         half, first, count = groups[g]
@@ -70,16 +78,47 @@
         whole = buf.at[half, pl.ds(0, blocks), pl.ds(first, count)]
         pltpu.make_async_copy(whole, whole, sem.at[g]).wait()
 
+    def columns(pair):
+        tall = jnp.concatenate([pair.astype(jnp.float32), jnp.zeros((SUB - 2, channels), jnp.float32)], axis=0).T
+        return [jnp.broadcast_to(tall[:, k:k + 1], (channels, wide)) for k in range(2)]
+
+    def prepare_in(update):
+        for k in range(4):
+            w_in[k * channels:(k + 1) * channels] = w_ab[update, :, k * channels:(k + 1) * channels].T
+        w_in[4 * channels:] = w_g[update].T
+        ln[0], ln[1] = columns(ln_z[update])
+
+    def prepare_out(update):
+        w_out[...] = w_o[update].T
+        ln[2], ln[3] = columns(ln_x[update])
+
+    def enter(half):
+        z_copies[half].wait()
+        for s in range(SUB):
+            base = half * 2 * SUB + s
+            block = jnp.concatenate([z_raw[base], z_raw[base + SUB]], axis=0)
+            z_out[:, half * half_lanes + s * LANES:half * half_lanes + (s + 1) * LANES] = block.T
+
+    def leave(half):
+        for s in range(SUB):
+            base = half * 2 * SUB + s
+            block = z_out[:, half * half_lanes + s * LANES:half * half_lanes + (s + 1) * LANES].T
+            z_raw[base] = block[:n_cols]
+            z_raw[base + SUB] = block[n_cols:]
+        z_outs[half].start()
+
+    z_outs = [pltpu.make_async_copy(z_raw.at[pl.ds(h * half_rows, half_rows)], out_hbm.at[pl.ds(h * half_rows, half_rows)], z_sem.at[h]) for h in range(HALVES)]
+
     def project(update, half):
-        gain = jnp.broadcast_to(ln[update, 0], (channels, wide))
-        bias = jnp.broadcast_to(ln[update, 1], (channels, wide))
-        weights = w_in[update, 0:4 * channels]
+        gain = ln[0]
+        bias = ln[1]
+        weights = w_in[:4 * channels]
         for n in range(half_lanes // wide):
             lanes = pl.ds(half * half_lanes + n * wide, wide)
             zn = norm_rows(z_out[:, lanes], gain, bias)
             z_norm[:, lanes] = zn
             q = jnp.dot(weights, zn, preferred_element_type=jnp.float32)
-            keep = 0.5 * mask[:, lanes]
+            keep = jnp.concatenate([mask[half, 2 * n + k:2 * n + k + 1] for k in range(2)], axis=1)
             a = (jnp.tanh(0.5 * q[channels:2 * channels]) + 1.0) * (keep * q[:channels])
             b = (jnp.tanh(0.5 * q[3 * channels:]) + 1.0) * (keep * q[2 * channels:3 * channels])
             for k in range(2):
@@ -91,8 +130,8 @@
         for d in range(n_dev):
             send_ab[half, d] = stage[d * rows:(d + 1) * rows, :].astype(jnp.bfloat16).reshape(per_dev, 2 * SUB, LANES)
 
-    def make_gate(update):
-        weights = w_in[update, 4 * channels:]
+    def make_gate():
+        weights = w_in[4 * channels:]
 
         def piece(n, carry):
             lanes = pl.ds(pl.multiple_of(n * wide, wide), wide)
@@ -100,7 +139,7 @@
             gate[:, lanes] = 0.5 * jnp.tanh(0.5 * v) + 0.5
             return carry
 
-        lax.fori_loop(0, z_in.shape[1] // wide, piece, 0, unroll=4)
+        lax.fori_loop(0, z_out.shape[1] // wide, piece, 0, unroll=4)
 
     low = lax.broadcasted_iota(jnp.int32, (SUB, LANES), 1) < LANES // 2
 
@@ -139,10 +178,10 @@
                         send_x[half, r * col_devs + 2 * h, c] = first
                         send_x[half, r * col_devs + 2 * h + 1, c] = second
 
-    def finish(update, half):
-        gain = jnp.broadcast_to(ln[update, 2], (channels, wide))
-        bias = jnp.broadcast_to(ln[update, 3], (channels, wide))
-        weights = w_out[update]
+    def finish(half):
+        gain = ln[2]
+        bias = ln[3]
+        weights = w_out[...]
         flat = recv_x.at[half].reshape(channels * SUB, LANES)
         for n in range(half_lanes // wide):
             lanes = pl.ds(half * half_lanes + n * wide, wide)
@@ -150,10 +189,20 @@
             y = jnp.dot(weights, norm_rows(x, gain, bias), preferred_element_type=jnp.float32)
             z_out[:, lanes] += gate[:, lanes] * y
 
-    z_out[...] = z_in[...]
+    for half in range(HALVES):
+        keep = 0.5 * mask_in[half * half_rows:(half + 1) * half_rows].astype(jnp.float32)
+        mask[half] = jnp.concatenate([keep[:SUB], keep[SUB:]], axis=1)
+    for copy in w_copies:
+        copy.wait()
+    prepare_in(0)
+    for half in range(HALVES):
+        enter(half)
+    pl.semaphore_wait(pltpu.get_barrier_semaphore(), n_dev - 1)
 
     def turn(update):
-        make_gate(update)
+        make_gate()
+        prepare_out(update)
+        prepare_in(jnp.minimum(update + 1, n_updates - 1))
         wait_group(recv_ab, ab_rsem, ab_groups, 0, n_dev)
         unpack(0)
         for g in range(2):
@@ -178,10 +227,12 @@
                 for g in range(3):
                     if x_groups[g][0] == half:
                         wait_group(recv_x, x_rsem, x_groups, g, n_dev)
-                finish(i - 1, half)
+                finish(half)
                 for g in range(3):
                     if ab_groups[g][0] == half:
                         wait_group(send_ab, ab_ssem, ab_groups, g, n_dev - 1)
+
+            pl.when(i == n_updates)(lambda: leave(half))
 
             @pl.when(i < n_updates)
             def _():
@@ -198,6 +249,8 @@
         return carry
 
     lax.fori_loop(0, n_updates + 1, step, 0)
+    for copy in z_outs:
+        copy.wait()
 
 
 def solution(mesh):
@@ -212,36 +265,42 @@
         positions = n_rows * n_cols
         n_updates = w_o.shape[0] * w_o.shape[1]
         per_dev = channels // n_dev
-        groups = (HALVES, 2, SUB, n_cols)
-        z_t = pair_act.reshape(*groups, channels).transpose(4, 0, 2, 1, 3).reshape(channels, positions)
-        mask = pair_mask.astype(jnp.float32).reshape(groups).transpose(0, 2, 1, 3).reshape(1, positions)
-        w_in = jnp.concatenate([w_ab, w_g], axis=-1).reshape(n_updates, channels, 5 * channels).swapaxes(1, 2)
-        w_out = w_o.reshape(n_updates, channels, channels).swapaxes(1, 2)
-        ln = jnp.concatenate([ln_z, ln_x], axis=2).astype(jnp.float32).reshape(n_updates, 4, channels, 1)
+        updates = lambda v: v.reshape(n_updates, *v.shape[2:])
         vmem = pl.BlockSpec(memory_space=pltpu.VMEM)
-        z_t = pl.pallas_call(
+        hbm = pl.BlockSpec(memory_space=pl.ANY)
+        f32, bf16 = jnp.float32, jnp.bfloat16
+        return pl.pallas_call(
             functools.partial(kernel, row_devs, col_devs, n_updates),
-            out_shape=jax.ShapeDtypeStruct((channels, positions), jnp.float32),
-            in_specs=[vmem] * 5,
-            out_specs=vmem,
+            out_shape=jax.ShapeDtypeStruct(pair_act.shape, f32),
+            in_specs=[hbm, vmem, vmem, hbm, hbm, vmem, hbm],
+            out_specs=hbm,
             scratch_shapes=[
-                pltpu.VMEM((channels, positions), jnp.bfloat16),
-                pltpu.VMEM((channels, positions), jnp.float32),
-                pltpu.VMEM((channels * 2 * SUB, LANES), jnp.float32),
-                pltpu.VMEM((HALVES, n_dev, per_dev, 2 * SUB, LANES), jnp.bfloat16),
-                pltpu.VMEM((HALVES, n_dev, per_dev, 2 * SUB, LANES), jnp.bfloat16),
-                pltpu.VMEM((per_dev, n_rows * row_devs, n_cols * col_devs), jnp.bfloat16),
-                pltpu.VMEM((per_dev, n_rows * row_devs, n_cols * col_devs), jnp.bfloat16),
-                pltpu.VMEM((HALVES, n_dev, per_dev, SUB, LANES), jnp.float32),
-                pltpu.VMEM((HALVES, n_dev, per_dev, SUB, LANES), jnp.float32),
-                pltpu.SemaphoreType.DMA((3,)),
-                pltpu.SemaphoreType.DMA((3,)),
-                pltpu.SemaphoreType.DMA((3,)),
+                pltpu.VMEM(pair_act.shape, f32),
+                pltpu.VMEM((n_updates, channels, 4 * channels), bf16),
+                pltpu.VMEM((n_updates, channels, channels), bf16),
+                pltpu.VMEM((n_updates, channels, channels), bf16),
+                pltpu.VMEM((5 * channels, channels), bf16),
+                pltpu.VMEM((channels, channels), bf16),
+                pltpu.VMEM((4, channels, 2 * LANES), f32),
+                pltpu.VMEM((HALVES, SUB, LANES), f32),
+                pltpu.VMEM((channels, positions), f32),
+                pltpu.VMEM((channels, positions), bf16),
+                pltpu.VMEM((channels, positions), f32),
+                pltpu.VMEM((channels * 2 * SUB, LANES), f32),
+                pltpu.VMEM((HALVES, n_dev, per_dev, 2 * SUB, LANES), bf16),
+                pltpu.VMEM((HALVES, n_dev, per_dev, 2 * SUB, LANES), bf16),
+                pltpu.VMEM((per_dev, n_rows * row_devs, n_cols * col_devs), bf16),
+                pltpu.VMEM((per_dev, n_rows * row_devs, n_cols * col_devs), bf16),
+                pltpu.VMEM((HALVES, n_dev, per_dev, SUB, LANES), f32),
+                pltpu.VMEM((HALVES, n_dev, per_dev, SUB, LANES), f32),
+                pltpu.SemaphoreType.DMA((3,)),
+                pltpu.SemaphoreType.DMA((3,)),
+                pltpu.SemaphoreType.DMA((3,)),
+                pltpu.SemaphoreType.DMA((3,)),
+                pltpu.SemaphoreType.DMA((HALVES,)),
                 pltpu.SemaphoreType.DMA((3,)),
             ],
-            compiler_params=pltpu.CompilerParams(collective_id=0, has_side_effects=True, vmem_limit_bytes=40 * 2**20),
-        )(z_t, mask, w_in, w_out, ln)
-        z = z_t.reshape(channels, HALVES, SUB, 2, n_cols).transpose(1, 3, 2, 4, 0)
-        return z.reshape(n_rows, n_cols, channels)
+            compiler_params=pltpu.CompilerParams(collective_id=0, has_side_effects=True, vmem_limit_bytes=60 * 2**20),
+        )(pair_act, pair_mask, updates(ln_z), updates(w_ab), updates(w_g), updates(ln_x), updates(w_o))
 
     return jax.shard_map(local_stack, mesh=mesh, in_specs=(pair_spec, mask_spec, P(), P(), P(), P(), P()), out_specs=pair_spec, check_vma=False)

time: 458 us -> 420 us (0.917)
  Pallas kernels: 435 us -> 417 us
  local copies, waits for them, and re-layouts: 18.9 us -> 2.31 us
    pallas_call x1, Pallas kernels: 435 us -> 417 us  [local_stack(): pl.pallas_call(functools.partial(kernel, row_devs, col_devs, n_updates),...]
    concatenate x3 -> x0, local copies, waits for them, and re-layouts: 5.64 us -> none  [the longest x1 3.22 us: local_stack(): jnp.concatenate([w_ab, w_g], axis=-1)]
where the time goes in v3:
time: 420 us
  Pallas kernels  417 us (99%)
    pallas_call x1, Pallas kernels, local_stack(): pl.pallas_call(functools.partial(kernel, row_devs, col_devs, n_updates),...  417 us

profile of v3, /device:TPU:97, one launch (start us, length us, event | category | flops | bytes accessed | tf_op | source)
XLA Modules:
  0.0 419.5 jit_solution(17489762537869691980)
XLA Ops:
  0.0 417.2 %shard_map.73 = f32[32,64,128]{2,1,0:T(8,128)} custom-call(f32[32,64,128]{2,1,0:T(8,128)} %z_hbm.1, s32[32,64]{1,0:T(8,128)} %mask_in.1, bf16[16,2,128]{2,1,0:T(2,128)(2,1)} %bitcast.8, bf16[16,128,512]{2,1,0:T(8,128)(2,1)} %bitcast.5, bf16[16,128,128]{2,1,0:T(8,128)(2,1)} %bitcast.6, bf16[16,2,128]{2,1,0:T(2,128)(2,1)} %bitcast.9, bf16[16,128,128]{2,1,0:T(8,128)(2,1)} %bitcast.7), custom_call_target="tpu_custom_call" | custom-call | tf_op jit(solution)/shard_map/pallas_call | solution.py:272
  417.2 2.3 copy.9

commit v4 on v3

--- a/solution.py
+++ b/solution.py
@@ -12,6 +12,7 @@
 HALVES = 2
 LANES = 128
 SUB = 8
+SPLIT = 4
 
 
 def norm_rows(values, gain, bias):
@@ -38,9 +39,8 @@
     half_rows = z_raw.shape[0] // HALVES
     n_cols = z_raw.shape[1]
     wide = 2 * LANES
-    part = per_dev // 2
-    ab_groups = ((0, 0, per_dev), (1, 0, part), (1, part, part))
-    x_groups = ((0, 0, part), (0, part, part), (1, 0, per_dev))
+    part = per_dev // SPLIT
+    groups = [(half, k * part, part) for half in range(HALVES) for k in range(SPLIT)]
     row = lax.axis_index("dap")
     col = lax.axis_index("dap2")
     me = row * col_devs + col
@@ -59,7 +59,7 @@
     for copy in z_copies + w_copies:
         copy.start()
 
-    def send_group(src, dst, ssem, rsem, groups, g):
+    def send_group(src, dst, ssem, rsem, g):
         half, first, count = groups[g]
         part_of = pl.ds(first, count)
         for other_row, other_col in peers:
@@ -73,7 +73,7 @@
             ).start()
         pltpu.make_async_copy(src.at[half, me, part_of], dst.at[half, me, part_of], rsem.at[g]).start()
 
-    def wait_group(buf, sem, groups, g, blocks):
+    def wait_group(buf, sem, g, blocks):
         half, first, count = groups[g]
         whole = buf.at[half, pl.ds(0, blocks), pl.ds(first, count)]
         pltpu.make_async_copy(whole, whole, sem.at[g]).wait()
@@ -150,7 +150,7 @@
         return jnp.where(low, first, swap(second)), jnp.where(low, swap(first), second)
 
     def unpack(g):
-        half, start, count = ab_groups[g]
+        half, start, count = groups[g]
 
         def channel(c, carry):
             for r in range(row_devs):
@@ -203,48 +203,49 @@
         make_gate()
         prepare_out(update)
         prepare_in(jnp.minimum(update + 1, n_updates - 1))
-        wait_group(recv_ab, ab_rsem, ab_groups, 0, n_dev)
-        unpack(0)
-        for g in range(2):
-            wait_group(recv_ab, ab_rsem, ab_groups, 1 + g, n_dev)
-            unpack(1 + g)
+        for k in range(SPLIT):
+            wait_group(recv_ab, ab_rsem, k, n_dev)
+            unpack(k)
+        for k in range(SPLIT):
+            wait_group(recv_ab, ab_rsem, SPLIT + k, n_dev)
+            unpack(SPLIT + k)
             @pl.when(update % 2 == 0)
             def _():
-                contract(True, g * part, part)
+                contract(True, k * part, part)
 
             @pl.when(update % 2 == 1)
             def _():
-                contract(False, g * part, part)
-
-            send_group(send_x, recv_x, x_ssem, x_rsem, x_groups, g)
-        send_group(send_x, recv_x, x_ssem, x_rsem, x_groups, 2)
+                contract(False, k * part, part)
+
+            send_group(send_x, recv_x, x_ssem, x_rsem, k)
+        for k in range(SPLIT):
+            send_group(send_x, recv_x, x_ssem, x_rsem, SPLIT + k)
 
     def step(i, carry):
         pl.when(i > 0)(lambda: turn(i - 1))
         for half in range(HALVES):
+            mine = range(half * SPLIT, (half + 1) * SPLIT)
+
             @pl.when(i > 0)
             def _():
-                for g in range(3):
-                    if x_groups[g][0] == half:
-                        wait_group(recv_x, x_rsem, x_groups, g, n_dev)
+                for g in mine:
+                    wait_group(recv_x, x_rsem, g, n_dev)
                 finish(half)
-                for g in range(3):
-                    if ab_groups[g][0] == half:
-                        wait_group(send_ab, ab_ssem, ab_groups, g, n_dev - 1)
+                for g in mine:
+                    wait_group(send_ab, ab_ssem, g, n_dev - 1)
 
             pl.when(i == n_updates)(lambda: leave(half))
 
             @pl.when(i < n_updates)
             def _():
                 project(i, half)
-                for g in range(3):
-                    if ab_groups[g][0] == half:
-                        send_group(send_ab, recv_ab, ab_ssem, ab_rsem, ab_groups, g)
+                for g in mine:
+                    send_group(send_ab, recv_ab, ab_ssem, ab_rsem, g)
 
         @pl.when(i > 0)
         def _():
-            for g in range(3):
-                wait_group(send_x, x_ssem, x_groups, g, n_dev - 1)
+            for g in range(len(groups)):
+                wait_group(send_x, x_ssem, g, n_dev - 1)
 
         return carry
 
@@ -293,12 +294,12 @@
                 pltpu.VMEM((per_dev, n_rows * row_devs, n_cols * col_devs), bf16),
                 pltpu.VMEM((HALVES, n_dev, per_dev, SUB, LANES), f32),
                 pltpu.VMEM((HALVES, n_dev, per_dev, SUB, LANES), f32),
-                pltpu.SemaphoreType.DMA((3,)),
-                pltpu.SemaphoreType.DMA((3,)),
-                pltpu.SemaphoreType.DMA((3,)),
-                pltpu.SemaphoreType.DMA((3,)),
+                pltpu.SemaphoreType.DMA((HALVES * SPLIT,)),
+                pltpu.SemaphoreType.DMA((HALVES * SPLIT,)),
+                pltpu.SemaphoreType.DMA((HALVES * SPLIT,)),
+                pltpu.SemaphoreType.DMA((HALVES * SPLIT,)),
                 pltpu.SemaphoreType.DMA((HALVES,)),
-                pltpu.SemaphoreType.DMA((3,)),
+                pltpu.SemaphoreType.DMA((HALVES * SPLIT,)),
             ],
             compiler_params=pltpu.CompilerParams(collective_id=0, has_side_effects=True, vmem_limit_bytes=60 * 2**20),
         )(pair_act, pair_mask, updates(ln_z), updates(w_ab), updates(w_g), updates(ln_x), updates(w_o))

time: 420 us -> 381 us (0.907)
  Pallas kernels: 417 us -> 379 us
    pallas_call x1, Pallas kernels: 417 us -> 379 us  [local_stack(): pl.pallas_call(functools.partial(kernel, row_devs, col_devs, n_updates),...]
where the time goes in v4:
time: 381 us
  Pallas kernels  379 us (99%)
    pallas_call x1, Pallas kernels, local_stack(): pl.pallas_call(functools.partial(kernel, row_devs, col_devs, n_updates),...  379 us

profile of v4, /device:TPU:97, one launch (start us, length us, event | category | flops | bytes accessed | tf_op | source)
XLA Modules:
  0.0 381.2 jit_solution(6902620475923972067)
XLA Ops:
  0.0 378.9 %shard_map.73 = f32[32,64,128]{2,1,0:T(8,128)} custom-call(f32[32,64,128]{2,1,0:T(8,128)} %z_hbm.1, s32[32,64]{1,0:T(8,128)} %mask_in.1, bf16[16,2,128]{2,1,0:T(2,128)(2,1)} %bitcast.8, bf16[16,128,512]{2,1,0:T(8,128)(2,1)} %bitcast.5, bf16[16,128,128]{2,1,0:T(8,128)(2,1)} %bitcast.6, bf16[16,2,128]{2,1,0:T(2,128)(2,1)} %bitcast.9, bf16[16,128,128]{2,1,0:T(8,128)(2,1)} %bitcast.7), custom_call_target="tpu_custom_call" | custom-call | tf_op jit(solution)/shard_map/pallas_call | solution.py:273
  378.9 2.3 copy.9

commit v5 on v4

--- a/solution.py
+++ b/solution.py
@@ -126,9 +126,13 @@
                 stage[pl.ds(sub, channels, stride=2 * SUB), :] = a[:, k * LANES:(k + 1) * LANES]
                 stage[pl.ds(SUB + sub, channels, stride=2 * SUB), :] = b[:, k * LANES:(k + 1) * LANES]
 
-        rows = per_dev * 2 * SUB
-        for d in range(n_dev):
-            send_ab[half, d] = stage[d * rows:(d + 1) * rows, :].astype(jnp.bfloat16).reshape(per_dev, 2 * SUB, LANES)
+        rows = 2 * SUB
+        for k in range(SPLIT):
+            for c in range(k * part, (k + 1) * part):
+                for d in range(n_dev):
+                    base = (d * per_dev + c) * rows
+                    send_ab[half, d, c] = stage[base:base + rows, :].astype(jnp.bfloat16)
+            send_group(send_ab, recv_ab, ab_ssem, ab_rsem, half * SPLIT + k)
 
     def make_gate():
         weights = w_in[4 * channels:]
@@ -239,8 +243,6 @@
             @pl.when(i < n_updates)
             def _():
                 project(i, half)
-                for g in mine:
-                    send_group(send_ab, recv_ab, ab_ssem, ab_rsem, g)
 
         @pl.when(i > 0)
         def _():

time: 381 us -> 381 us (level)
  no operation moved by 1% of the time
where the time goes in v5:
time: 381 us
  Pallas kernels  379 us (99%)
    pallas_call x1, Pallas kernels, local_stack(): pl.pallas_call(functools.partial(kernel, row_devs, col_devs, n_updates),...  379 us

profile of v5, /device:TPU:97, one launch (start us, length us, event | category | flops | bytes accessed | tf_op | source)
XLA Modules:
  0.0 381.2 jit_solution(3488026053693316611)
XLA Ops:
  0.0 378.9 %shard_map.73 = f32[32,64,128]{2,1,0:T(8,128)} custom-call(f32[32,64,128]{2,1,0:T(8,128)} %z_hbm.1, s32[32,64]{1,0:T(8,128)} %mask_in.1, bf16[16,2,128]{2,1,0:T(2,128)(2,1)} %bitcast.8, bf16[16,128,512]{2,1,0:T(8,128)(2,1)} %bitcast.5, bf16[16,128,128]{2,1,0:T(8,128)(2,1)} %bitcast.6, bf16[16,2,128]{2,1,0:T(2,128)(2,1)} %bitcast.9, bf16[16,128,128]{2,1,0:T(8,128)(2,1)} %bitcast.7), custom_call_target="tpu_custom_call" | custom-call | tf_op jit(solution)/shard_map/pallas_call | solution.py:275
  378.9 2.3 copy.9
